TPU v7x, 32 devices: a whole 2x2x4 slice. The times are simulated.
32 devices in a mesh: rep: 2 (over y), gx: 4 (over x, core), gy: 4 (over z).
Axes of the slice: x: 2, y: 2, z: 4, core: 2. Of those that a mesh axis runs over, the one named last changes fastest.
Arguments:
- deltas: bfloat16 [2, 2, 3584, 14336], P('rep', None, 'gx', 'gy'), may hold values from -32 to 32
- params: float32 [2, 4, 4, 2, 4, 4, 112, 896], P(None, None, 'gx', 'rep', None, 'gy'), may hold values from -0.75 to 0.75
- momentum: float32 [2, 4, 4, 2, 4, 4, 112, 896], P(None, None, 'gx', 'rep', None, 'gy'), may hold values from -1.5 to 1.5
Outputs:
- new_params: float32 [2, 4, 4, 2, 4, 4, 112, 896], P(None, None, 'gx', 'rep', None, 'gy')
- new_momentum: float32 [2, 4, 4, 2, 4, 4, 112, 896], P(None, None, 'gx', 'rep', None, 'gy')
All inputs are finite; a program needn't handle non-finite values.
Results may differ from a plain program's by a relative error of at most 0.0003.
Values may be sent and summed in bfloat16 or wider, within the bound.
A program may use at most 128 MiB of HBM per device.

v0:
```python
import functools

import jax
import jax.numpy as jnp
from jax import lax
from jax.experimental import pallas as pl
from jax.experimental.pallas import tpu as pltpu
from jax.sharding import PartitionSpec as P

clip_level = 0.25
moment_decay = 0.9
outer_rate = 0.7
epsilon = 1e-06

MESH = pl.DeviceIdType.MESH
LANES = 128
TOP = 240.0
SMALLEST = 1e-30
AHEAD = 16
LARGE = 54 * 1024 * 1024


def encode(value):
    power = value * value
    for _ in range(3):
        power = power * power
    return jnp.where(value < 0.0, -power, power).astype(jnp.bfloat16)


def decode(code):
    wide = code.astype(jnp.float32)
    root = jnp.exp2(jnp.log2(jnp.abs(wide)) * (1.0 / 16.0))
    root = jnp.where(wide == 0.0, 0.0, root)
    return jnp.where(wide < 0.0, -root, root)


def fold_lanes(tile, combine):
    folded = tile[:, :LANES]
    for start in range(LANES, tile.shape[1], LANES):
        folded = combine(folded, tile[:, start : start + LANES])
    return folded


def exchange(
    replicas, rows_split, cols_split, matrices,
    delta_ref, tiles_ref, peaks_ref, squares_ref,
    own, peer, stage, peaks, wide, total, mine, from_rep, middle, from_grid,
    own_sem, rep_send, rep_recv, tile_send, tile_recv, peak_send, peak_recv,
    first_send, first_recv, second_send, second_recv, local_sem,
):
    rep, gx, gy = lax.axis_index("rep"), lax.axis_index("gx"), lax.axis_index("gy")
    steps, rows, cols = stage.shape
    grid = rows_split * cols_split
    far = rows_split * (cols_split - 1)
    remote_steps = steps - matrices
    band = total.shape[0]
    here = gx * cols_split + gy

    def place(step):
        turn, matrix = step // matrices, step % matrices
        spread = max(cols_split - 1, 1)
        is_far = turn < far
        row_shift = jnp.where(is_far, turn // spread, (turn - far + 1) % rows_split)
        col_shift = jnp.where(is_far, 1 + (turn % spread + 1) % spread, 0)
        return matrix, (gx + row_shift) % rows_split, (gy + col_shift) % cols_split

    def block(step, replica):
        matrix, c, d = place(step)
        return delta_ref.at[matrix, c, replica, :, pl.ds(pl.multiple_of(d * cols, LANES), cols)]

    def own_copy(step):
        return pltpu.make_async_copy(block(step, rep), own.at[step], own_sem.at[step])

    def rep_copy(shift, step):
        target = (rep + shift) % replicas
        return pltpu.make_async_remote_copy(
            src_ref=block(step, target), dst_ref=peer.at[shift - 1, step],
            send_sem=rep_send.at[shift - 1, step], recv_sem=rep_recv.at[shift - 1, step],
            device_id={"rep": target}, device_id_type=MESH,
        )

    def tile_copies(step):
        matrix, c, d = place(step)
        slot = here * matrices + matrix
        target = {"gx": c, "gy": d}
        return (
            pltpu.make_async_remote_copy(
                src_ref=stage.at[step], dst_ref=tiles_ref.at[matrix, gx, gy],
                send_sem=tile_send.at[step], recv_sem=tile_recv.at[slot],
                device_id=target, device_id_type=MESH,
            ),
            pltpu.make_async_remote_copy(
                src_ref=peaks.at[step], dst_ref=peaks_ref.at[matrix, gx, gy],
                send_sem=peak_send.at[step], recv_sem=peak_recv.at[slot],
                device_id=target, device_id_type=MESH,
            ),
        )

    def neighbour(shift):
        return (gx + shift // cols_split) % rows_split, (gy + shift % cols_split) % cols_split

    barrier = pltpu.get_barrier_semaphore()
    for shift in range(1, replicas):
        pl.semaphore_signal(
            barrier, inc=1, device_id={"rep": (rep + shift) % replicas}, device_id_type=MESH
        )

    def greet(shift, carry):
        c, d = neighbour(shift)
        pl.semaphore_signal(barrier, inc=1, device_id={"gx": c, "gy": d}, device_id_type=MESH)
        return carry

    lax.fori_loop(1, grid, greet, 0)
    pl.semaphore_wait(barrier, replicas - 1 + grid - 1)

    def launch(step):
        own_copy(step).start()
        for shift in range(1, replicas):
            rep_copy(shift, step).start()

    ahead = min(AHEAD, steps)
    lax.fori_loop(0, ahead, lambda step, carry: (launch(step), carry)[1], 0)
    total[...] = jnp.zeros_like(total)

    def advance(step, carry):
        own_copy(step).wait()
        for shift in range(1, replicas):
            rep_copy(shift, step).wait_recv()

        @pl.when(step + ahead < steps)
        def _():
            launch(step + ahead)

        def average(index, peak):
            at = pl.ds(pl.multiple_of(index * band, band), band)
            value = own[step, at, :].astype(jnp.float32)
            for shift in range(1, replicas):
                value = value + peer[shift - 1, step, at, :].astype(jnp.float32)
            value = value * (1.0 / replicas)
            total[...] += value * value
            wide[at, :] = value
            return jnp.maximum(peak, fold_lanes(jnp.abs(value), jnp.maximum))

        peak = lax.fori_loop(0, rows // band, average, jnp.zeros((band, LANES), jnp.float32))
        peak = jnp.maximum(jnp.max(peak, axis=0, keepdims=True), SMALLEST)
        peaks[step] = peak * (1.0 / TOP)
        lift = jnp.concatenate([TOP / peak] * (cols // LANES), axis=1)

        def code(index, carry):
            at = pl.ds(pl.multiple_of(index * band, band), band)
            stage[step, at, :] = encode(wide[at, :] * lift)
            return carry

        lax.fori_loop(0, rows // band, code, 0)

        @pl.when(step < remote_steps)
        def _():
            for copy in tile_copies(step):
                copy.start()

        return carry

    lax.fori_loop(0, steps, advance, 0)

    mine[...] = jnp.sum(fold_lanes(total[...], jnp.add), axis=0, keepdims=True)

    def local_copies(matrix):
        step = remote_steps + matrix
        return (
            pltpu.make_async_copy(stage.at[step], tiles_ref.at[matrix, gx, gy], local_sem.at[matrix, 0]),
            pltpu.make_async_copy(peaks.at[step], peaks_ref.at[matrix, gx, gy], local_sem.at[matrix, 1]),
        )

    def first_copy(shift):
        return pltpu.make_async_remote_copy(
            src_ref=mine, dst_ref=from_rep.at[shift - 1],
            send_sem=first_send.at[shift - 1], recv_sem=first_recv.at[shift - 1],
            device_id={"rep": (rep + shift) % replicas}, device_id_type=MESH,
        )

    def second_copy(shift):
        c, d = neighbour(shift)
        return pltpu.make_async_remote_copy(
            src_ref=middle, dst_ref=from_grid.at[shift - 1],
            send_sem=second_send.at[shift - 1], recv_sem=second_recv.at[shift - 1],
            device_id={"gx": c, "gy": d}, device_id_type=MESH,
        )

    for matrix in range(matrices):
        for copy in local_copies(matrix):
            copy.start()
    for shift in range(1, replicas):
        first_copy(shift).start()
    for matrix in range(matrices):
        for copy in local_copies(matrix):
            copy.wait()
    subtotal = mine[...]
    for shift in range(1, replicas):
        first_copy(shift).wait()
        subtotal = subtotal + from_rep[shift - 1]
    middle[...] = subtotal

    def close_rep(step, carry):
        for shift in range(1, replicas):
            rep_copy(shift, step).wait_send()
        return carry

    lax.fori_loop(0, steps, close_rep, 0)
    lax.fori_loop(1, grid, lambda shift, carry: (second_copy(shift).start(), carry)[1], 0)

    def gather(shift, carry):
        second_copy(shift).wait()
        return carry + from_grid[shift - 1]

    squares_ref[...] = lax.fori_loop(1, grid, gather, subtotal)

    def close_send(step, carry):
        for copy in tile_copies(step):
            copy.wait_send()
        return carry

    lax.fori_loop(0, remote_steps, close_send, 0)

    def close_recv(index, carry):
        c, d = neighbour(1 + index // matrices)
        matrix = index % matrices
        slot = (c * cols_split + d) * matrices + matrix
        target = {"gx": c, "gy": d}
        pltpu.make_async_remote_copy(
            src_ref=stage.at[0], dst_ref=tiles_ref.at[matrix, c, d],
            send_sem=tile_send.at[0], recv_sem=tile_recv.at[slot],
            device_id=target, device_id_type=MESH,
        ).wait_recv()
        pltpu.make_async_remote_copy(
            src_ref=peaks.at[0], dst_ref=peaks_ref.at[matrix, c, d],
            send_sem=peak_send.at[0], recv_sem=peak_recv.at[slot],
            device_id=target, device_id_type=MESH,
        ).wait_recv()
        return carry

    lax.fori_loop(0, remote_steps, close_recv, 0)


def update(entries, squares_ref, tiles_ref, peaks_ref, params_ref, momentum_ref, new_params_ref, new_momentum_ref):
    squares = jnp.sum(squares_ref[...], axis=1, keepdims=True)
    clip_scale = jnp.minimum(1.0, clip_level / jnp.sqrt(squares / entries + epsilon))
    count, rows, cols = tiles_ref.shape
    band = 16 if rows % 16 == 0 else rows
    for tile in range(count):
        lift = jnp.concatenate([peaks_ref[tile] * clip_scale] * (cols // LANES), axis=1)

        for start in range(0, rows, band):
            at = slice(start, start + band)
            gradient = decode(tiles_ref[tile, at, :]) * lift
            new_momentum = moment_decay * momentum_ref[tile, at, :] + gradient
            new_momentum_ref[tile, at, :] = new_momentum
            new_params_ref[tile, at, :] = params_ref[tile, at, :] - outer_rate * (
                gradient + moment_decay * new_momentum
            )


def per_device(deltas, params, momentum):
    rows_split = lax.axis_size("gx")
    cols_split = lax.axis_size("gy")
    replicas = lax.axis_size("rep")
    matrices, local_rows, local_cols = deltas.shape[1:]
    rows = local_rows // (rows_split * replicas)
    cols = local_cols // cols_split
    entries = matrices * local_rows * local_cols * rows_split * cols_split
    grid = rows_split * cols_split
    steps = grid * matrices
    remote_steps = steps - matrices
    band = 16 if rows % 16 == 0 else rows
    any_space = pl.BlockSpec(memory_space=pl.ANY)
    vmem = pl.BlockSpec(memory_space=pltpu.VMEM)
    dma = pltpu.SemaphoreType.DMA
    f32, bf16 = jnp.float32, jnp.bfloat16
    tiles, peaks, squares = pl.pallas_call(
        functools.partial(exchange, replicas, rows_split, cols_split, matrices),
        out_shape=(
            jax.ShapeDtypeStruct((matrices, rows_split, cols_split, rows, cols), bf16),
            jax.ShapeDtypeStruct((matrices, rows_split, cols_split, 1, LANES), f32),
            jax.ShapeDtypeStruct((1, LANES), f32),
        ),
        in_specs=[any_space],
        out_specs=(any_space, any_space, vmem),
        scratch_shapes=[
            pltpu.VMEM((steps, rows, cols), bf16),
            pltpu.VMEM((max(replicas - 1, 1), steps, rows, cols), bf16),
            pltpu.VMEM((steps, rows, cols), bf16),
            pltpu.VMEM((steps, 1, LANES), f32),
            pltpu.VMEM((rows, cols), f32),
            pltpu.VMEM((band, cols), f32),
            pltpu.VMEM((1, LANES), f32),
            pltpu.VMEM((max(replicas - 1, 1), 1, LANES), f32),
            pltpu.VMEM((1, LANES), f32),
            pltpu.VMEM((grid, 1, LANES), f32),
            dma((steps,)),
            dma((max(replicas - 1, 1), steps)),
            dma((max(replicas - 1, 1), steps)),
            dma((steps,)),
            dma((steps,)),
            dma((steps,)),
            dma((steps,)),
            dma((max(replicas - 1, 1),)),
            dma((max(replicas - 1, 1),)),
            dma((grid,)),
            dma((grid,)),
            dma((matrices, 2)),
        ],
        compiler_params=pltpu.CompilerParams(
            collective_id=0, has_side_effects=True, vmem_limit_bytes=LARGE
        ),
    )(deltas.reshape(matrices, rows_split, replicas, rows, local_cols))
    tile_shape = (steps, rows, cols)
    count = 2 if steps % 2 == 0 else 1
    whole = pl.BlockSpec((1, LANES), lambda i: (0, 0))
    tile_block = pl.BlockSpec((count, rows, cols), lambda i: (i, 0, 0))
    peak_block = pl.BlockSpec((count, 1, LANES), lambda i: (i, 0, 0))
    wide_shape = jax.ShapeDtypeStruct(tile_shape, f32)
    new_params, new_momentum = pl.pallas_call(
        functools.partial(update, entries),
        grid=(steps // count,),
        out_shape=(wide_shape, wide_shape),
        in_specs=[whole, tile_block, peak_block, tile_block, tile_block],
        out_specs=(tile_block, tile_block),
        compiler_params=pltpu.CompilerParams(vmem_limit_bytes=LARGE),
    )(
        squares,
        tiles.reshape(tile_shape),
        peaks.reshape(steps, 1, LANES),
        params.reshape(tile_shape),
        momentum.reshape(tile_shape),
    )
    return (new_params.reshape(params.shape), new_momentum.reshape(momentum.shape))


def solution(mesh):
    placement = P(None, None, "gx", "rep", None, "gy", None, None)
    return jax.shard_map(
        per_device,
        mesh=mesh,
        in_specs=(P("rep", None, "gx", "gy"), placement, placement),
        out_specs=(placement, placement),
        check_vma=False,
    )
```

profile of v0, /device:TPU:0, one launch (start us, length us, event | category | flops | bytes accessed | tf_op | source)
XLA Modules:
  0.0 183.8 jit_solution(15746523399981148285)
XLA Ops:
  0.6 157.0 %shard_map.50 = (bf16[2,4,4,112,896]{4,3,2,1,0:T(8,128)(2,1)}, f32[2,4,4,1,128]{4,3,2,1,0:T(1,128)}, f32[1,128]{1,0:T(1,128)}) custom-call(bf16[2,4,2,112,3584]{4,3,2,1,0:T(8,128)(2,1)} %bitcast.11), custom_call_target="tpu_custom_call" | custom-call | tf_op jit(solution)/shard_map/pallas_call | solution.py:278
  157.6 26.2 %shard_map.51 = (f32[32,112,896]{2,1,0:T(8,128)}, f32[32,112,896]{2,1,0:T(8,128)}) custom-call(f32[1,128]{1,0:T(1,128)} %get-tuple-element.7.squares_ref, bf16[32,112,896]{2,1,0:T(8,128)(2,1)} %bitcast.14, f32[32,1,128]{2,1,0:T(1,128)} %bitcast.15, f32[32,112,896]{2,1,0:T(8,128)} %bitcast.12, f32[32,112,896]{2,1,0:T(8,128)} %bitcast.13), custom_call_target="tpu_custom_call" | custom-call | tf_op jit(solution)/shard_map/pallas_call | solution.py:321
where the time goes:
time: 184 us
  Pallas kernels  183 us (99%)
    pallas_call x1, Pallas kernels, per_device(): pl.pallas_call(functools.partial(exchange, replicas, rows_split, cols_spl...  157 us
    pallas_call x1, Pallas kernels, per_device(): pl.pallas_call(functools.partial(update, entries), grid=(steps // count,)...  26.2 us

commit v1 on v0

v1 whole, which is shorter than its diff:
```python
import functools

import jax
import jax.numpy as jnp
from jax import lax
from jax.experimental import pallas as pl
from jax.experimental.pallas import tpu as pltpu
from jax.sharding import PartitionSpec as P

clip_level = 0.25
moment_decay = 0.9
outer_rate = 0.7
epsilon = 1e-06

MESH = pl.DeviceIdType.MESH
LANES = 128
TOP = 240.0
SMALLEST = 1e-30
SLOTS = 4
PREFETCH_AT = 2
EXCHANGE_VMEM = 22 * 1024 * 1024
UPDATE_VMEM = 14 * 1024 * 1024


def encode(value):
    power = value * value
    for _ in range(3):
        power = power * power
    return jnp.where(value < 0.0, -power, power).astype(jnp.bfloat16)


def decode(code):
    wide = code.astype(jnp.float32)
    root = jnp.exp2(jnp.log2(jnp.abs(wide)) * (1.0 / 16.0))
    root = jnp.where(wide == 0.0, 0.0, root)
    return jnp.where(wide < 0.0, -root, root)


def fold_lanes(tile, combine):
    folded = tile[:, :LANES]
    for start in range(LANES, tile.shape[1], LANES):
        folded = combine(folded, tile[:, start : start + LANES])
    return folded


def exchange(
    replicas, rows_split, cols_split, matrices,
    delta_ref, params_ref, momentum_ref, state_ref,
    own, peer, landed, peaks, landed_peaks, wide, total, mine, from_rep, middle, from_grid,
    own_sem, rep_send, rep_recv, tile_send, tile_recv, peak_send, peak_recv,
    first_send, first_recv, second_send, second_recv, state_sem,
):
    rep, gx, gy = lax.axis_index("rep"), lax.axis_index("gx"), lax.axis_index("gy")
    steps, rows, cols = own.shape
    grid = rows_split * cols_split
    far = rows_split * (cols_split - 1)
    far_steps = far * matrices
    remote_steps = steps - matrices
    band = total.shape[0]
    spread = max(cols_split - 1, 1)

    def place(step, sign):
        turn, matrix = step // matrices, step % matrices
        is_far = turn < far
        row_shift = jnp.where(is_far, turn // spread, (turn - far + 1) % rows_split)
        col_shift = jnp.where(is_far, 1 + (turn % spread + 1) % spread, 0)
        c = (gx + rows_split + sign * row_shift) % rows_split
        d = (gy + cols_split + sign * col_shift) % cols_split
        return matrix, c, d

    def block(step, replica):
        matrix, c, d = place(step, 1)
        return delta_ref.at[matrix, c, replica, :, pl.ds(pl.multiple_of(d * cols, LANES), cols)]

    def own_copy(step):
        return pltpu.make_async_copy(block(step, rep), own.at[step], own_sem.at[step])

    def rep_copy(shift, step):
        target = (rep + shift) % replicas
        return pltpu.make_async_remote_copy(
            src_ref=block(step, target), dst_ref=peer.at[shift - 1, step],
            send_sem=rep_send.at[shift - 1, step], recv_sem=rep_recv.at[shift - 1, step],
            device_id={"rep": target}, device_id_type=MESH,
        )

    def tile_copies(step):
        matrix, c, d = place(step, 1)
        target = {"gx": c, "gy": d}
        return (
            pltpu.make_async_remote_copy(
                src_ref=own.at[step], dst_ref=landed.at[step],
                send_sem=tile_send.at[step], recv_sem=tile_recv.at[step],
                device_id=target, device_id_type=MESH,
            ),
            pltpu.make_async_remote_copy(
                src_ref=peaks.at[step], dst_ref=landed_peaks.at[step],
                send_sem=peak_send.at[step], recv_sem=peak_recv.at[step],
                device_id=target, device_id_type=MESH,
            ),
        )

    def neighbour(shift):
        return (gx + shift // cols_split) % rows_split, (gy + shift % cols_split) % cols_split

    def state_copies():
        return (
            pltpu.make_async_copy(params_ref, state_ref.at[pl.ds(steps, steps)], state_sem.at[0]),
            pltpu.make_async_copy(momentum_ref, state_ref.at[pl.ds(2 * steps, steps)], state_sem.at[1]),
        )

    barrier = pltpu.get_barrier_semaphore()
    for shift in range(1, replicas):
        pl.semaphore_signal(
            barrier, inc=1, device_id={"rep": (rep + shift) % replicas}, device_id_type=MESH
        )

    def greet(shift, carry):
        c, d = neighbour(shift)
        pl.semaphore_signal(barrier, inc=1, device_id={"gx": c, "gy": d}, device_id_type=MESH)
        return carry

    lax.fori_loop(1, grid, greet, 0)
    pl.semaphore_wait(barrier, replicas - 1 + grid - 1)

    def launch(step, carry):
        own_copy(step).start()
        for shift in range(1, replicas):
            rep_copy(shift, step).start()
        return carry

    lax.fori_loop(0, steps, launch, 0)
    total[...] = jnp.zeros_like(total)

    def spot(matrix, c, d):
        return (matrix * rows_split + c) * cols_split + d

    def band_at(index):
        return pl.ds(pl.multiple_of(index * band, band), band)

    def mean_of(step, at):
        value = own[step, at, :].astype(jnp.float32)
        for shift in range(1, replicas):
            value = value + peer[shift - 1, step, at, :].astype(jnp.float32)
        value = value * (1.0 / replicas)
        total[...] += value * value
        return value

    def arrive(step):
        own_copy(step).wait()
        for shift in range(1, replicas):
            rep_copy(shift, step).wait_recv()

    def unpack(step):
        for copy in tile_copies(step):
            copy.wait_recv()
        matrix, c, d = place(step, -1)
        lift = jnp.concatenate([landed_peaks[step]] * (cols // LANES), axis=1)

        def part(index, carry):
            at = band_at(index)
            state_ref[spot(matrix, c, d), at, :] = decode(landed[step, at, :]) * lift
            return carry

        lax.fori_loop(0, rows // band, part, 0)

    def ready(step):
        return jnp.clip((3 * step - 8) // 4, 0, far_steps)

    def advance(step, carry):
        arrive(step)

        def average(index, peak):
            at = band_at(index)
            value = mean_of(step, at)
            wide[at, :] = value
            return jnp.maximum(peak, fold_lanes(jnp.abs(value), jnp.maximum))

        peak = lax.fori_loop(0, rows // band, average, jnp.zeros((band, LANES), jnp.float32))
        peak = jnp.maximum(jnp.max(peak, axis=0, keepdims=True), SMALLEST)
        peaks[step] = peak * (1.0 / TOP)
        lift = jnp.concatenate([TOP / peak] * (cols // LANES), axis=1)

        def code(index, carry):
            at = band_at(index)
            own[step, at, :] = encode(wide[at, :] * lift)
            return carry

        lax.fori_loop(0, rows // band, code, 0)
        for copy in tile_copies(step):
            copy.start()

        @pl.when(step == PREFETCH_AT)
        def _():
            for copy in state_copies():
                copy.start()

        @pl.when(ready(step) > ready(step - 1))
        def _():
            unpack(ready(step) - 1)

        @pl.when(step >= far_steps + 3)
        def _():
            unpack(step - 3)

        return carry

    lax.fori_loop(0, remote_steps, advance, 0)

    def keep(step, carry):
        arrive(step)
        matrix = step - remote_steps

        def average(index, inner):
            at = band_at(index)
            state_ref[spot(matrix, gx, gy), at, :] = mean_of(step, at)
            return inner

        return lax.fori_loop(0, rows // band, average, carry)

    lax.fori_loop(remote_steps, steps, keep, 0)

    mine[...] = jnp.sum(fold_lanes(total[...], jnp.add), axis=0, keepdims=True)

    def first_copy(shift):
        return pltpu.make_async_remote_copy(
            src_ref=mine, dst_ref=from_rep.at[shift - 1],
            send_sem=first_send.at[shift - 1], recv_sem=first_recv.at[shift - 1],
            device_id={"rep": (rep + shift) % replicas}, device_id_type=MESH,
        )

    def second_copy(shift):
        c, d = neighbour(shift)
        return pltpu.make_async_remote_copy(
            src_ref=middle, dst_ref=from_grid.at[shift - 1],
            send_sem=second_send.at[shift - 1], recv_sem=second_recv.at[shift - 1],
            device_id={"gx": c, "gy": d}, device_id_type=MESH,
        )

    for shift in range(1, replicas):
        first_copy(shift).start()
    subtotal = mine[...]
    for shift in range(1, replicas):
        first_copy(shift).wait()
        subtotal = subtotal + from_rep[shift - 1]
    middle[...] = subtotal
    lax.fori_loop(1, grid, lambda shift, carry: (second_copy(shift).start(), carry)[1], 0)

    last = ready(remote_steps - 1)
    lax.fori_loop(last, far_steps, lambda step, carry: (unpack(step), carry)[1], 0)
    lax.fori_loop(
        max(remote_steps - 3, far_steps), remote_steps, lambda step, carry: (unpack(step), carry)[1], 0
    )
    for copy in state_copies():
        copy.wait()

    def close_rep(step, carry):
        for shift in range(1, replicas):
            rep_copy(shift, step).wait_send()
        return carry

    lax.fori_loop(0, steps, close_rep, 0)

    def close_send(step, carry):
        for copy in tile_copies(step):
            copy.wait_send()
        return carry

    lax.fori_loop(0, remote_steps, close_send, 0)

    def gather(shift, carry):
        second_copy(shift).wait()
        return carry + from_grid[shift - 1]

    state_ref[3 * steps, :1, :LANES] = lax.fori_loop(1, grid, gather, subtotal)


def update(entries, state_ref, new_params_ref, new_momentum_ref, params_out, momentum_out, sems):
    count, (rows, cols) = state_ref.shape[0] // 3, state_ref.shape[1:]
    squares = jnp.sum(state_ref[3 * count, :1, :LANES], axis=1, keepdims=True)
    clip_scale = jnp.minimum(1.0, clip_level / jnp.sqrt(squares / entries + epsilon))
    band = 8 if rows % 8 == 0 else rows

    def copies(tile):
        slot = tile % SLOTS
        return (
            pltpu.make_async_copy(params_out.at[slot], new_params_ref.at[tile], sems.at[0, slot]),
            pltpu.make_async_copy(momentum_out.at[slot], new_momentum_ref.at[tile], sems.at[1, slot]),
        )

    def one(tile, carry):
        slot = tile % SLOTS

        @pl.when(tile >= SLOTS)
        def _():
            for copy in copies(tile - SLOTS):
                copy.wait()

        def part(index, inner):
            at = pl.ds(pl.multiple_of(index * band, band), band)
            gradient = state_ref[tile, at, :] * clip_scale
            new_momentum = moment_decay * state_ref[2 * count + tile, at, :] + gradient
            momentum_out[slot, at, :] = new_momentum
            params_out[slot, at, :] = state_ref[count + tile, at, :] - outer_rate * (
                gradient + moment_decay * new_momentum
            )
            return inner

        lax.fori_loop(0, rows // band, part, 0, unroll=2 if (rows // band) % 2 == 0 else 1)
        for copy in copies(tile):
            copy.start()
        return carry

    lax.fori_loop(0, count, one, 0)

    def close(tile, carry):
        for copy in copies(tile):
            copy.wait()
        return carry

    lax.fori_loop(max(count - SLOTS, 0), count, close, 0)


def per_device(deltas, params, momentum):
    rows_split = lax.axis_size("gx")
    cols_split = lax.axis_size("gy")
    replicas = lax.axis_size("rep")
    matrices, local_rows, local_cols = deltas.shape[1:]
    rows = local_rows // (rows_split * replicas)
    cols = local_cols // cols_split
    entries = matrices * local_rows * local_cols * rows_split * cols_split
    grid = rows_split * cols_split
    steps = grid * matrices
    band = 16 if rows % 16 == 0 else rows
    any_space = pl.BlockSpec(memory_space=pl.ANY)
    vmem = pl.BlockSpec(memory_space=pltpu.VMEM)
    dma = pltpu.SemaphoreType.DMA
    f32, bf16 = jnp.float32, jnp.bfloat16
    flat_shape = (steps, rows, cols)
    state = pl.pallas_call(
        functools.partial(exchange, replicas, rows_split, cols_split, matrices),
        out_shape=pltpu.VMEM((3 * steps + 1, rows, cols), f32),
        in_specs=[any_space] * 3,
        out_specs=vmem,
        scratch_shapes=[
            pltpu.VMEM(flat_shape, bf16),
            pltpu.VMEM((max(replicas - 1, 1), *flat_shape), bf16),
            pltpu.VMEM(flat_shape, bf16),
            pltpu.VMEM((steps, 1, LANES), f32),
            pltpu.VMEM((steps, 1, LANES), f32),
            pltpu.VMEM((rows, cols), f32),
            pltpu.VMEM((band, cols), f32),
            pltpu.VMEM((1, LANES), f32),
            pltpu.VMEM((max(replicas - 1, 1), 1, LANES), f32),
            pltpu.VMEM((1, LANES), f32),
            pltpu.VMEM((grid, 1, LANES), f32),
            dma((steps,)),
            dma((max(replicas - 1, 1), steps)),
            dma((max(replicas - 1, 1), steps)),
            dma((steps,)),
            dma((steps,)),
            dma((steps,)),
            dma((steps,)),
            dma((max(replicas - 1, 1),)),
            dma((max(replicas - 1, 1),)),
            dma((grid,)),
            dma((grid,)),
            dma((2,)),
        ],
        compiler_params=pltpu.CompilerParams(
            collective_id=0, has_side_effects=True, vmem_limit_bytes=EXCHANGE_VMEM
        ),
    )(
        deltas.reshape(matrices, rows_split, replicas, rows, local_cols),
        params.reshape(flat_shape),
        momentum.reshape(flat_shape),
    )
    wide_shape = jax.ShapeDtypeStruct(flat_shape, f32)
    new_params, new_momentum = pl.pallas_call(
        functools.partial(update, entries),
        out_shape=(wide_shape, wide_shape),
        in_specs=[vmem],
        out_specs=(any_space, any_space),
        scratch_shapes=[
            pltpu.VMEM((SLOTS, rows, cols), f32),
            pltpu.VMEM((SLOTS, rows, cols), f32),
            dma((2, SLOTS)),
        ],
        compiler_params=pltpu.CompilerParams(vmem_limit_bytes=UPDATE_VMEM),
    )(pltpu.with_memory_space_constraint(state, pltpu.VMEM))
    return (new_params.reshape(params.shape), new_momentum.reshape(momentum.shape))


def solution(mesh):
    placement = P(None, None, "gx", "rep", None, "gy", None, None)
    return jax.shard_map(
        per_device,
        mesh=mesh,
        in_specs=(P("rep", None, "gx", "gy"), placement, placement),
        out_specs=(placement, placement),
        check_vma=False,
    )
```

time: 184 us -> 171 us (0.929); the launches traced: 184 us -> 168 us
  Pallas kernels: 183 us -> 168 us
    pallas_call x1, Pallas kernels: 26.2 us -> 9.05 us  [per_device(): pl.pallas_call(functools.partial(update, entries), out_shape=(wide_shape,...]
where the time goes in v1:
time: 171 us; the launch traced here: 168 us
  Pallas kernels  168 us (98%)
    pallas_call x1, Pallas kernels, per_device(): pl.pallas_call(functools.partial(exchange, replicas, rows_split, cols_spl...  159 us
    pallas_call x1, Pallas kernels, per_device(): pl.pallas_call(functools.partial(update, entries), out_shape=(wide_shape,...  9.05 us

profile of v1, /device:TPU:0, one launch (start us, length us, event | category | flops | bytes accessed | tf_op | source)
XLA Modules:
  0.0 168.2 jit_solution(9508626594363814820)
XLA Ops:
  0.6 158.6 %shard_map.50.state_ref = f32[97,112,896]{2,1,0:T(8,128)S(1)} custom-call(bf16[2,4,2,112,3584]{4,3,2,1,0:T(8,128)(2,1)} %bitcast.9, f32[32,112,896]{2,1,0:T(8,128)} %bitcast.10, f32[32,112,896]{2,1,0:T(8,128)} %bitcast.11), custom_call_target="tpu_custom_call" | custom-call | tf_op jit(solution)/shard_map/pallas_call | solution.py:339
  159.2 9.0 %shard_map.51 = (f32[32,112,896]{2,1,0:T(8,128)}, f32[32,112,896]{2,1,0:T(8,128)}) custom-call(f32[97,112,896]{2,1,0:T(8,128)S(1)} %shard_map.50.state_ref), custom_call_target="tpu_custom_call" | custom-call | tf_op jit(solution)/shard_map/pallas_call | solution.py:378

commit v2 on v1

--- a/solution.py
+++ b/solution.py
@@ -16,10 +16,12 @@
 LANES = 128
 TOP = 240.0
 SMALLEST = 1e-30
-SLOTS = 4
-PREFETCH_AT = 2
+SLOTS = 12
+PREFETCH_AT = 4
+READY_LAG = 21
+NEAR_LAG = 5
 EXCHANGE_VMEM = 22 * 1024 * 1024
-UPDATE_VMEM = 14 * 1024 * 1024
+UPDATE_VMEM = 20 * 1024 * 1024
 
 
 def encode(value):
@@ -46,24 +48,30 @@
 def exchange(
     replicas, rows_split, cols_split, matrices,
     delta_ref, params_ref, momentum_ref, state_ref,
-    own, peer, landed, peaks, landed_peaks, wide, total, mine, from_rep, middle, from_grid,
+    first, own, peer, landed, peaks, landed_peaks, wide, total, mine, from_all,
     own_sem, rep_send, rep_recv, tile_send, tile_recv, peak_send, peak_recv,
-    first_send, first_recv, second_send, second_recv, state_sem,
+    squares_send, squares_recv, state_sem, first_sem, met,
 ):
     rep, gx, gy = lax.axis_index("rep"), lax.axis_index("gx"), lax.axis_index("gy")
     steps, rows, cols = own.shape
-    grid = rows_split * cols_split
+    devices = replicas * rows_split * cols_split
     far = rows_split * (cols_split - 1)
     far_steps = far * matrices
     remote_steps = steps - matrices
     band = total.shape[0]
-    spread = max(cols_split - 1, 1)
+    spread, half = max(cols_split - 1, 1), cols_split // 2
+    pieces = rows // band
+
+    def band_at(index):
+        return pl.ds(pl.multiple_of(index * band, band), band)
 
     def place(step, sign):
         turn, matrix = step // matrices, step % matrices
         is_far = turn < far
         row_shift = jnp.where(is_far, turn // spread, (turn - far + 1) % rows_split)
-        col_shift = jnp.where(is_far, 1 + (turn % spread + 1) % spread, 0)
+        col_shift = jnp.where(turn % spread < half, turn % spread, turn % spread + 1)
+        col_shift = jnp.where(turn % spread == 0, half, col_shift)
+        col_shift = jnp.where(is_far, col_shift, 0)
         c = (gx + rows_split + sign * row_shift) % rows_split
         d = (gy + cols_split + sign * col_shift) % cols_split
         return matrix, c, d
@@ -74,6 +82,41 @@
 
     def own_copy(step):
         return pltpu.make_async_copy(block(step, rep), own.at[step], own_sem.at[step])
+
+    def own_piece(piece):
+        at = band_at(piece)
+        return pltpu.make_async_copy(block(0, rep).at[at], own.at[0, at], own_sem.at[steps + piece])
+
+    def first_piece(shift, piece):
+        at = band_at(piece)
+        target = (rep + shift) % replicas
+        return pltpu.make_async_copy(block(0, target).at[at], first.at[shift - 1, at], first_sem.at[shift - 1, piece])
+
+    def rep_piece(shift, piece):
+        at = band_at(piece)
+        target = (rep + shift) % replicas
+        return pltpu.make_async_remote_copy(
+            src_ref=first.at[shift - 1, at], dst_ref=peer.at[shift - 1, 0, at],
+            send_sem=rep_send.at[shift - 1, steps + piece], recv_sem=rep_recv.at[shift - 1, steps + piece],
+            device_id={"rep": target}, device_id_type=MESH,
+        )
+
+    def tile_pieces(piece):
+        _, c, d = place(0, 1)
+        at = band_at(piece)
+        target = {"gx": c, "gy": d}
+        return (
+            pltpu.make_async_remote_copy(
+                src_ref=own.at[0, at], dst_ref=landed.at[0, at],
+                send_sem=tile_send.at[steps + piece], recv_sem=tile_recv.at[steps + piece],
+                device_id=target, device_id_type=MESH,
+            ),
+            pltpu.make_async_remote_copy(
+                src_ref=peaks.at[steps + piece], dst_ref=landed_peaks.at[steps + piece],
+                send_sem=peak_send.at[steps + piece], recv_sem=peak_recv.at[steps + piece],
+                device_id=target, device_id_type=MESH,
+            ),
+        )
 
     def rep_copy(shift, step):
         target = (rep + shift) % replicas
@@ -99,8 +142,16 @@
             ),
         )
 
-    def neighbour(shift):
-        return (gx + shift // cols_split) % rows_split, (gy + shift % cols_split) % cols_split
+    def other(shift):
+        place = ((gy * rows_split + gx) * replicas + rep + shift) % devices
+        return {"gy": place // (rows_split * replicas), "gx": place // replicas % rows_split, "rep": place % replicas}
+
+    def squares_copy(shift):
+        return pltpu.make_async_remote_copy(
+            src_ref=mine, dst_ref=from_all.at[shift - 1],
+            send_sem=squares_send.at[shift - 1], recv_sem=squares_recv.at[shift - 1],
+            device_id=other(shift), device_id_type=MESH,
+        )
 
     def state_copies():
         return (
@@ -108,34 +159,62 @@
             pltpu.make_async_copy(momentum_ref, state_ref.at[pl.ds(2 * steps, steps)], state_sem.at[1]),
         )
 
+    def fetch_piece(piece, carry):
+        for shift in range(1, replicas):
+            first_piece(shift, piece).start()
+        own_piece(piece).start()
+        return carry
+
+    lax.fori_loop(0, pieces, fetch_piece, 0)
+
+    def greet_near(semaphore):
+        for shift in range(1, rows_split):
+            pl.semaphore_signal(
+                semaphore, inc=1, device_id={"gx": (gx + shift) % rows_split}, device_id_type=MESH
+            )
+
+        @pl.when(gy > 0)
+        def _():
+            pl.semaphore_signal(semaphore, inc=1, device_id={"gy": gy - 1}, device_id_type=MESH)
+
+        @pl.when(gy < cols_split - 1)
+        def _():
+            pl.semaphore_signal(semaphore, inc=1, device_id={"gy": gy + 1}, device_id_type=MESH)
+
+    def greet_peers(semaphore):
+        for shift in range(1, replicas):
+            pl.semaphore_signal(
+                semaphore, inc=1, device_id={"rep": (rep + shift) % replicas}, device_id_type=MESH
+            )
+
+    near = rows_split - 1 + (gy > 0).astype(jnp.int32) + (gy < cols_split - 1).astype(jnp.int32)
     barrier = pltpu.get_barrier_semaphore()
-    for shift in range(1, replicas):
-        pl.semaphore_signal(
-            barrier, inc=1, device_id={"rep": (rep + shift) % replicas}, device_id_type=MESH
-        )
-
-    def greet(shift, carry):
-        c, d = neighbour(shift)
-        pl.semaphore_signal(barrier, inc=1, device_id={"gx": c, "gy": d}, device_id_type=MESH)
-        return carry
-
-    lax.fori_loop(1, grid, greet, 0)
-    pl.semaphore_wait(barrier, replicas - 1 + grid - 1)
+    greet_peers(barrier)
+    greet_near(barrier)
+    pl.semaphore_wait(barrier, replicas - 1 + near)
 
     def launch(step, carry):
-        own_copy(step).start()
         for shift in range(1, replicas):
             rep_copy(shift, step).start()
         return carry
 
-    lax.fori_loop(0, steps, launch, 0)
+    def launch_piece(piece, carry):
+        for shift in range(1, replicas):
+            first_piece(shift, piece).wait()
+            rep_piece(shift, piece).start()
+        return carry
+
+    lax.fori_loop(0, pieces, launch_piece, 0)
+    lax.fori_loop(1, steps, launch, 0)
+    for relay in range(cols_split - 1):
+        greet_near(met.at[relay])
+        pl.semaphore_wait(met.at[relay], near)
+    greet_peers(met.at[cols_split - 1])
+    lax.fori_loop(1, steps, lambda step, carry: (own_copy(step).start(), carry)[1], 0)
     total[...] = jnp.zeros_like(total)
 
     def spot(matrix, c, d):
         return (matrix * rows_split + c) * cols_split + d
-
-    def band_at(index):
-        return pl.ds(pl.multiple_of(index * band, band), band)
 
     def mean_of(step, at):
         value = own[step, at, :].astype(jnp.float32)
@@ -163,8 +242,34 @@
 
         lax.fori_loop(0, rows // band, part, 0)
 
+    def unpack_pieces():
+        matrix, c, d = place(0, -1)
+
+        def part(piece, carry):
+            for copy in tile_pieces(piece):
+                copy.wait_recv()
+            at = band_at(piece)
+            lift = jnp.concatenate([landed_peaks[steps + piece]] * (cols // LANES), axis=1)
+            state_ref[spot(matrix, c, d), at, :] = decode(landed[0, at, :]) * lift
+            return carry
+
+        lax.fori_loop(0, pieces, part, 0)
+
     def ready(step):
-        return jnp.clip((3 * step - 8) // 4, 0, far_steps)
+        return jnp.clip((3 * step - READY_LAG) // 4, 0, far_steps)
+
+    def unpack_some(step):
+        @pl.when((ready(step) > ready(step - 1)) & (ready(step) > 1))
+        def _():
+            unpack(ready(step) - 1)
+
+        @pl.when(step >= far_steps + NEAR_LAG)
+        def _():
+            unpack(step - NEAR_LAG)
+
+    def scales(peak):
+        peak = jnp.maximum(jnp.max(peak, axis=0, keepdims=True), SMALLEST)
+        return peak * (1.0 / TOP), jnp.concatenate([TOP / peak] * (cols // LANES), axis=1)
 
     def advance(step, carry):
         arrive(step)
@@ -176,9 +281,7 @@
             return jnp.maximum(peak, fold_lanes(jnp.abs(value), jnp.maximum))
 
         peak = lax.fori_loop(0, rows // band, average, jnp.zeros((band, LANES), jnp.float32))
-        peak = jnp.maximum(jnp.max(peak, axis=0, keepdims=True), SMALLEST)
-        peaks[step] = peak * (1.0 / TOP)
-        lift = jnp.concatenate([TOP / peak] * (cols // LANES), axis=1)
+        peaks[step], lift = scales(peak)
 
         def code(index, carry):
             at = band_at(index)
@@ -191,22 +294,30 @@
 
         @pl.when(step == PREFETCH_AT)
         def _():
+            unpack_pieces()
             for copy in state_copies():
                 copy.start()
 
-        @pl.when(ready(step) > ready(step - 1))
-        def _():
-            unpack(ready(step) - 1)
-
-        @pl.when(step >= far_steps + 3)
-        def _():
-            unpack(step - 3)
-
-        return carry
-
-    lax.fori_loop(0, remote_steps, advance, 0)
+        unpack_some(step)
+        return carry
+
+    def open_piece(piece, carry):
+        own_piece(piece).wait()
+        for shift in range(1, replicas):
+            rep_piece(shift, piece).wait_recv()
+        at = band_at(piece)
+        value = mean_of(0, at)
+        peaks[steps + piece], lift = scales(fold_lanes(jnp.abs(value), jnp.maximum))
+        own[0, at, :] = encode(value * lift)
+        for copy in tile_pieces(piece):
+            copy.start()
+        return carry
+
+    lax.fori_loop(0, pieces, open_piece, 0)
+    lax.fori_loop(1, remote_steps, advance, 0)
 
     def keep(step, carry):
+        unpack_some(step)
         arrive(step)
         matrix = step - remote_steps
 
@@ -221,34 +332,13 @@
 
     mine[...] = jnp.sum(fold_lanes(total[...], jnp.add), axis=0, keepdims=True)
 
-    def first_copy(shift):
-        return pltpu.make_async_remote_copy(
-            src_ref=mine, dst_ref=from_rep.at[shift - 1],
-            send_sem=first_send.at[shift - 1], recv_sem=first_recv.at[shift - 1],
-            device_id={"rep": (rep + shift) % replicas}, device_id_type=MESH,
-        )
-
-    def second_copy(shift):
-        c, d = neighbour(shift)
-        return pltpu.make_async_remote_copy(
-            src_ref=middle, dst_ref=from_grid.at[shift - 1],
-            send_sem=second_send.at[shift - 1], recv_sem=second_recv.at[shift - 1],
-            device_id={"gx": c, "gy": d}, device_id_type=MESH,
-        )
-
-    for shift in range(1, replicas):
-        first_copy(shift).start()
-    subtotal = mine[...]
-    for shift in range(1, replicas):
-        first_copy(shift).wait()
-        subtotal = subtotal + from_rep[shift - 1]
-    middle[...] = subtotal
-    lax.fori_loop(1, grid, lambda shift, carry: (second_copy(shift).start(), carry)[1], 0)
-
-    last = ready(remote_steps - 1)
+    pl.semaphore_wait(met.at[cols_split - 1], replicas - 1)
+    lax.fori_loop(1, devices, lambda shift, carry: (squares_copy(shift).start(), carry)[1], 0)
+
+    last = ready(steps - 1)
     lax.fori_loop(last, far_steps, lambda step, carry: (unpack(step), carry)[1], 0)
     lax.fori_loop(
-        max(remote_steps - 3, far_steps), remote_steps, lambda step, carry: (unpack(step), carry)[1], 0
+        max(steps - NEAR_LAG, far_steps), remote_steps, lambda step, carry: (unpack(step), carry)[1], 0
     )
     for copy in state_copies():
         copy.wait()
@@ -258,20 +348,28 @@
             rep_copy(shift, step).wait_send()
         return carry
 
-    lax.fori_loop(0, steps, close_rep, 0)
+    def close_piece(piece, carry):
+        for shift in range(1, replicas):
+            rep_piece(shift, piece).wait_send()
+        for copy in tile_pieces(piece):
+            copy.wait_send()
+        return carry
+
+    lax.fori_loop(0, pieces, close_piece, 0)
+    lax.fori_loop(1, steps, close_rep, 0)
 
     def close_send(step, carry):
         for copy in tile_copies(step):
             copy.wait_send()
         return carry
 
-    lax.fori_loop(0, remote_steps, close_send, 0)
+    lax.fori_loop(1, remote_steps, close_send, 0)
 
     def gather(shift, carry):
-        second_copy(shift).wait()
-        return carry + from_grid[shift - 1]
-
-    state_ref[3 * steps, :1, :LANES] = lax.fori_loop(1, grid, gather, subtotal)
+        squares_copy(shift).wait()
+        return carry + from_all[shift - 1]
+
+    state_ref[3 * steps, :1, :LANES] = lax.fori_loop(1, devices, gather, mine[...])
 
 
 def update(entries, state_ref, new_params_ref, new_momentum_ref, params_out, momentum_out, sems):
@@ -329,8 +427,10 @@
     cols = local_cols // cols_split
     entries = matrices * local_rows * local_cols * rows_split * cols_split
     grid = rows_split * cols_split
+    devices = grid * replicas
     steps = grid * matrices
     band = 16 if rows % 16 == 0 else rows
+    pieces = rows // band
     any_space = pl.BlockSpec(memory_space=pl.ANY)
     vmem = pl.BlockSpec(memory_space=pltpu.VMEM)
     dma = pltpu.SemaphoreType.DMA
@@ -342,29 +442,28 @@
         in_specs=[any_space] * 3,
         out_specs=vmem,
         scratch_shapes=[
+            pltpu.VMEM((max(replicas - 1, 1), rows, cols), bf16),
             pltpu.VMEM(flat_shape, bf16),
             pltpu.VMEM((max(replicas - 1, 1), *flat_shape), bf16),
             pltpu.VMEM(flat_shape, bf16),
-            pltpu.VMEM((steps, 1, LANES), f32),
-            pltpu.VMEM((steps, 1, LANES), f32),
+            pltpu.VMEM((steps + pieces, 1, LANES), f32),
+            pltpu.VMEM((steps + pieces, 1, LANES), f32),
             pltpu.VMEM((rows, cols), f32),
             pltpu.VMEM((band, cols), f32),
             pltpu.VMEM((1, LANES), f32),
-            pltpu.VMEM((max(replicas - 1, 1), 1, LANES), f32),
-            pltpu.VMEM((1, LANES), f32),
-            pltpu.VMEM((grid, 1, LANES), f32),
-            dma((steps,)),
-            dma((max(replicas - 1, 1), steps)),
-            dma((max(replicas - 1, 1), steps)),
-            dma((steps,)),
-            dma((steps,)),
-            dma((steps,)),
-            dma((steps,)),
-            dma((max(replicas - 1, 1),)),
-            dma((max(replicas - 1, 1),)),
-            dma((grid,)),
-            dma((grid,)),
+            pltpu.VMEM((devices, 1, LANES), f32),
+            dma((steps + pieces,)),
+            dma((max(replicas - 1, 1), steps + pieces)),
+            dma((max(replicas - 1, 1), steps + pieces)),
+            dma((steps + pieces,)),
+            dma((steps + pieces,)),
+            dma((steps + pieces,)),
+            dma((steps + pieces,)),
+            dma((devices,)),
+            dma((devices,)),
             dma((2,)),
+            dma((max(replicas - 1, 1), pieces)),
+            pltpu.SemaphoreType.REGULAR((cols_split,)),
         ],
         compiler_params=pltpu.CompilerParams(
             collective_id=0, has_side_effects=True, vmem_limit_bytes=EXCHANGE_VMEM
@@ -381,9 +480,9 @@
         in_specs=[vmem],
         out_specs=(any_space, any_space),
         scratch_shapes=[
-            pltpu.VMEM((SLOTS, rows, cols), f32),
-            pltpu.VMEM((SLOTS, rows, cols), f32),
-            dma((2, SLOTS)),
+            pltpu.VMEM((min(SLOTS, steps), rows, cols), f32),
+            pltpu.VMEM((min(SLOTS, steps), rows, cols), f32),
+            dma((2, min(SLOTS, steps))),
         ],
         compiler_params=pltpu.CompilerParams(vmem_limit_bytes=UPDATE_VMEM),
     )(pltpu.with_memory_space_constraint(state, pltpu.VMEM))

time: 171 us -> 165 us (0.965); the launches traced: 168 us -> 164 us
  Pallas kernels: 168 us -> 164 us
    pallas_call x1, Pallas kernels: 159 us -> 155 us  [per_device(): pl.pallas_call(functools.partial(exchange, replicas, rows_split, cols_spl...]
where the time goes in v2:
time: 165 us; the launch traced here: 164 us
  Pallas kernels  164 us (99%)
    pallas_call x1, Pallas kernels, per_device(): pl.pallas_call(functools.partial(exchange, replicas, rows_split, cols_spl...  155 us
    pallas_call x1, Pallas kernels, per_device(): pl.pallas_call(functools.partial(update, entries), out_shape=(wide_shape,...  8.91 us

profile of v2, /device:TPU:0, one launch (start us, length us, event | category | flops | bytes accessed | tf_op | source)
XLA Modules:
  0.0 164.4 jit_solution(16780038020986088025)
XLA Ops:
  0.6 154.8 %shard_map.50.state_ref = f32[97,112,896]{2,1,0:T(8,128)S(1)} custom-call(bf16[2,4,2,112,3584]{4,3,2,1,0:T(8,128)(2,1)} %bitcast.9, f32[32,112,896]{2,1,0:T(8,128)} %bitcast.10, f32[32,112,896]{2,1,0:T(8,128)} %bitcast.11), custom_call_target="tpu_custom_call" | custom-call | tf_op jit(solution)/shard_map/pallas_call | solution.py:439
  155.4 8.9 %shard_map.51 = (f32[32,112,896]{2,1,0:T(8,128)}, f32[32,112,896]{2,1,0:T(8,128)}) custom-call(f32[97,112,896]{2,1,0:T(8,128)S(1)} %shard_map.50.state_ref), custom_call_target="tpu_custom_call" | custom-call | tf_op jit(solution)/shard_map/pallas_call | solution.py:477

commit v3 on v2

--- a/solution.py
+++ b/solution.py
@@ -59,6 +59,7 @@
     far_steps = far * matrices
     remote_steps = steps - matrices
     band = total.shape[0]
+    group = rows_split * matrices
     spread, half = max(cols_split - 1, 1), cols_split // 2
     pieces = rows // band
 
@@ -335,35 +336,38 @@
     pl.semaphore_wait(met.at[cols_split - 1], replicas - 1)
     lax.fori_loop(1, devices, lambda shift, carry: (squares_copy(shift).start(), carry)[1], 0)
 
+    early = max(far_steps - group, 1)
+    def close_rep(step, carry):
+        for shift in range(1, replicas):
+            rep_copy(shift, step).wait_send()
+        return carry
+
+    def close_piece(piece, carry):
+        for shift in range(1, replicas):
+            rep_piece(shift, piece).wait_send()
+        for copy in tile_pieces(piece):
+            copy.wait_send()
+        return carry
+
+    lax.fori_loop(0, pieces, close_piece, 0)
+    lax.fori_loop(1, steps, close_rep, 0)
+
+    def close_send(step, carry):
+        for copy in tile_copies(step):
+            copy.wait_send()
+        return carry
+
+    lax.fori_loop(1, early, close_send, 0)
+
     last = ready(steps - 1)
-    lax.fori_loop(last, far_steps, lambda step, carry: (unpack(step), carry)[1], 0)
     lax.fori_loop(
         max(steps - NEAR_LAG, far_steps), remote_steps, lambda step, carry: (unpack(step), carry)[1], 0
     )
+    lax.fori_loop(last, far_steps, lambda step, carry: (unpack(step), carry)[1], 0)
     for copy in state_copies():
         copy.wait()
 
-    def close_rep(step, carry):
-        for shift in range(1, replicas):
-            rep_copy(shift, step).wait_send()
-        return carry
-
-    def close_piece(piece, carry):
-        for shift in range(1, replicas):
-            rep_piece(shift, piece).wait_send()
-        for copy in tile_pieces(piece):
-            copy.wait_send()
-        return carry
-
-    lax.fori_loop(0, pieces, close_piece, 0)
-    lax.fori_loop(1, steps, close_rep, 0)
-
-    def close_send(step, carry):
-        for copy in tile_copies(step):
-            copy.wait_send()
-        return carry
-
-    lax.fori_loop(1, remote_steps, close_send, 0)
+    lax.fori_loop(early, remote_steps, close_send, 0)
 
     def gather(shift, carry):
         squares_copy(shift).wait()

time: 165 us -> 165 us (level)
  no operation moved by 1% of the time
where the time goes in v3:
time: 165 us; the launch traced here: 164 us
  Pallas kernels  164 us (99%)
    pallas_call x1, Pallas kernels, per_device(): pl.pallas_call(functools.partial(exchange, replicas, rows_split, cols_spl...  155 us
    pallas_call x1, Pallas kernels, per_device(): pl.pallas_call(functools.partial(update, entries), out_shape=(wide_shape,...  8.91 us

profile of v3, /device:TPU:0, one launch (start us, length us, event | category | flops | bytes accessed | tf_op | source)
XLA Modules:
  0.0 164.4 jit_solution(1148814526451470326)
XLA Ops:
  0.6 154.8 %shard_map.50.state_ref = f32[97,112,896]{2,1,0:T(8,128)S(1)} custom-call(bf16[2,4,2,112,3584]{4,3,2,1,0:T(8,128)(2,1)} %bitcast.9, f32[32,112,896]{2,1,0:T(8,128)} %bitcast.10, f32[32,112,896]{2,1,0:T(8,128)} %bitcast.11), custom_call_target="tpu_custom_call" | custom-call | tf_op jit(solution)/shard_map/pallas_call | solution.py:443
  155.4 8.9 %shard_map.51 = (f32[32,112,896]{2,1,0:T(8,128)}, f32[32,112,896]{2,1,0:T(8,128)}) custom-call(f32[97,112,896]{2,1,0:T(8,128)S(1)} %shard_map.50.state_ref), custom_call_target="tpu_custom_call" | custom-call | tf_op jit(solution)/shard_map/pallas_call | solution.py:481
